TPU v7x, 32 devices: a whole 2x2x4 slice. The times are simulated.
32 devices in a mesh: seq: 8 (over z, x), feat: 4 (over y, core).
Axes of the slice: x: 2, y: 2, z: 4, core: 2. Of those that a mesh axis runs over, the one named last changes fastest.
Arguments:
- injection: bfloat16 [1024, 5120], P('seq', 'feat'), may hold values from -8 to 8
- warm_start: bfloat16 [1024, 5120], P('seq', 'feat'), may hold values from -12 to 12
- gain_in: float32 [5120], replicated, may hold values from 0.5 to 1.5
- gain_out: float32 [5120], replicated, may hold values from 0.5 to 1.5
- w_query: bfloat16 [5120, 5120], P(None, 'feat'), may hold values from -0.0848993624 to 0.0848993624
- w_key: bfloat16 [5120, 1024], P(None, 'feat'), may hold values from -0.0848993624 to 0.0848993624
- w_value: bfloat16 [5120, 1024], P(None, 'feat'), may hold values from -0.078125 to 0.078125
- w_out: bfloat16 [5120, 5120], P('feat'), may hold values from -0.078125 to 0.078125
Outputs:
- equilibrium: float32 [1024, 5120], P('seq', 'feat')
All inputs are finite; a program needn't handle non-finite values.
Results may differ from a plain program's by a relative error of at most 0.009.
Values may be sent and summed in bfloat16 or wider, within the bound.
A program may use at most 128 MiB of HBM per device.

v0:
```python
import math
import jax
import jax.numpy as jnp
from jax import lax
from jax.sharding import PartitionSpec as P

HEADS = 40
KV_HEADS = 8
HEAD_DIM = 128
ITERS = 4
EPS = 1e-06
LAMBDA = 0.03


def solve_small(matrix, target):
    size_now = target.shape[0]
    row_list = [matrix[idx_row] for idx_row in range(size_now)]
    value_list = [target[idx_row] for idx_row in range(size_now)]
    for pivot_at in range(size_now):
        for below_at in range(pivot_at + 1, size_now):
            ratio_now = row_list[below_at][pivot_at] / row_list[pivot_at][pivot_at]
            row_list[below_at] = row_list[below_at] - ratio_now * row_list[pivot_at]
            value_list[below_at] = value_list[below_at] - ratio_now * value_list[pivot_at]
    result_list = [None] * size_now
    for pivot_at in reversed(range(size_now)):
        running = value_list[pivot_at]
        for later_at in range(pivot_at + 1, size_now):
            running = running - row_list[pivot_at][later_at] * result_list[later_at]
        result_list[pivot_at] = running / row_list[pivot_at][pivot_at]
    return jnp.stack(result_list)


def coefficients(gram_matrix, scale_all):
    history_len = gram_matrix.shape[0]
    system = gram_matrix / scale_all + LAMBDA * jnp.eye(history_len, dtype=jnp.float32)
    unscaled = solve_small(system, jnp.ones((history_len,), jnp.float32))
    return unscaled / jnp.sum(unscaled)


def on_device(injection, warm_start, gain_in, gain_out, w_query, w_key, w_value, w_out):
    seq_at = lax.axis_index("seq")
    tok_dev = injection.shape[0]
    width = gain_in.shape[0]
    head_cols = w_query.shape[1]
    kv_cols = w_key.shape[1]
    kv_local = kv_cols // HEAD_DIM
    group = HEADS // KV_HEADS
    scale_all = float(tok_dev * lax.axis_size("seq") * width)
    score_scale = 1.0 / math.sqrt(HEAD_DIM)
    w_joined = jnp.concatenate([w_query, w_key, w_value], axis=1)
    query_pos = seq_at * tok_dev + jnp.arange(tok_dev, dtype=jnp.int32)
    injection_here, start_here = (
        lax.all_to_all(injection, "feat", split_axis=0, concat_axis=1, tiled=True),
        lax.all_to_all(warm_start, "feat", split_axis=0, concat_axis=1, tiled=True),
    )
    injection_full = injection_here.astype(jnp.float32)
    current = start_here.astype(jnp.float32)
    evaluated = []
    residuals = []
    for iteration in range(ITERS):
        mixed = current + injection_full
        normed = (
            mixed * lax.rsqrt(jnp.mean(mixed * mixed, axis=1, keepdims=True) + EPS) * gain_in
        ).astype(jnp.bfloat16)
        layer_joined = jnp.dot(
            lax.all_gather(normed, "feat", axis=0, tiled=True),
            w_joined,
            preferred_element_type=jnp.float32,
        ).astype(jnp.bfloat16)
        queries = layer_joined[:, :head_cols].reshape(tok_dev, kv_local, group, HEAD_DIM)
        key_rows = layer_joined[:, head_cols : head_cols + kv_cols]
        value_rows = layer_joined[:, head_cols + kv_cols :]
        start_max = jnp.full((tok_dev, kv_local, group), -1e30, jnp.float32)
        run_max = start_max
        key_piece = lax.all_gather(key_rows, "seq", axis=0, tiled=True)
        value_piece = lax.all_gather(value_rows, "seq", axis=0, tiled=True)
        length = key_piece.shape[0]
        key_heads = key_piece.reshape(length, kv_local, HEAD_DIM)
        value_heads = value_piece.reshape(length, kv_local, HEAD_DIM)
        scores = (
            jnp.einsum("tkgd,skd->tkgs", queries, key_heads, preferred_element_type=jnp.float32)
            * score_scale
        )
        key_pos = jnp.arange(length, dtype=jnp.int32)
        allowed = (query_pos[:, None] >= key_pos[None, :])[:, None, None, :]
        scores = jnp.where(allowed, scores, -1e30)
        new_max = jnp.maximum(run_max, jnp.max(scores, axis=3))
        weights = jnp.where(allowed, jnp.exp(scores - new_max[..., None]), 0.0)
        run_sum = jnp.sum(weights, axis=3)
        run_acc = jnp.einsum(
            "tkgs,skd->tkgd",
            weights.astype(jnp.bfloat16),
            value_heads,
            preferred_element_type=jnp.float32,
        )
        run_max, run_sum, run_acc = (new_max, run_sum, run_acc)
        attended = (run_acc / run_sum[..., None]).astype(jnp.bfloat16).reshape(tok_dev, head_cols)
        update = lax.psum_scatter(
            jnp.dot(attended, w_out, preferred_element_type=jnp.float32),
            "feat",
            scatter_dimension=0,
            tiled=True,
        )
        summed = mixed + update
        image = (
            summed * lax.rsqrt(jnp.mean(summed * summed, axis=1, keepdims=True) + EPS) * gain_out
        )
        evaluated.append(image)
        residuals.append(image - current)
        if iteration == 0:
            current = image
        else:
            history_len = iteration + 1
            stacked = jnp.stack(residuals).reshape(history_len, -1)
            local_gram = jnp.dot(stacked, stacked.T, precision=lax.Precision.HIGHEST)
            gram_matrix = lax.psum(local_gram, ("seq", "feat"))
            weights_now = coefficients(gram_matrix, scale_all)
            current = weights_now[0] * evaluated[0]
            for other in range(1, history_len):
                current = current + weights_now[other] * evaluated[other]
    return lax.all_to_all(current, "feat", split_axis=1, concat_axis=0, tiled=True)


def solution(mesh):
    in_specs = (
        P("seq", "feat"),
        P("seq", "feat"),
        P(),
        P(),
        P(None, "feat"),
        P(None, "feat"),
        P(None, "feat"),
        P("feat", None),
    )
    out_specs = P("seq", "feat")
    return jax.shard_map(
        on_device, mesh=mesh, in_specs=in_specs, out_specs=out_specs, check_vma=False
    )
```

profile of v0, /device:TPU:0, one launch (start us, length us, event | category | flops | bytes accessed | tf_op | source)
XLA Modules:
  0.0 838.7 jit_solution(10279321022507677067)
XLA Ops:
  6.5 11.1 %all_to_all.45 = bf16[4,32,1280]{2,1,0:T(8,128)(2,1)S(1)} all-to-all(bf16[4,32,1280]{2,1,0:T(8,128)(2,1)} %bitcast.259), channel_id=1, replica_groups=mesh['seq'=8,'feat'=4] {'feat'}, dimensions={0} | all-to-all | bytes 655360 | tf_op jit(solution)/shard_map/all_to_all | solution.py:53
  17.6 3.5 all-to-all-start
  21.3 6.5 all-to-all-done
  29.1 10.9 %constant_dynamic-update-slice_fusion.2 = bf16[5120,1792]{1,0:T(8,128)(2,1)} fusion(bf16[5120,1280]{1,0:T(8,128)(2,1)} %param.12), kind=kLoop, calls=%fused_computation.95 | loop fusion | bytes 26214400
  40.0 3.6 constant_dynamic-update-slice_fusion.1
  48.3 9.2 %convolution_convert_fusion.3 = bf16[128,1792]{1,0:T(8,128)(2,1)S(1)} fusion(bf16[128,5120]{1,0:T(8,128)(2,1)} %all-gather.5.cloned.1.call-done, bf16[5120,1792]{1,0:T(8,128)(2,1)} %constant_dynamic-update-slice_fusion), kind=kOutput, calls=%fused_computation.36 | convolution fusion | flops 2349039616 | bytes 20119552 | tf_op jit(solution)/shard_map/dot_general | solution.py:65
  58.2 31.4 %all_gather.37 = bf16[1024,256]{1,0:T(8,128)(2,1)S(1)} all-gather(bf16[128,256]{1,0:T(8,128)(2,1)S(1)} %get-tuple-element.30), channel_id=1, replica_groups=mesh['seq'=8,'feat'=4] {'seq'}, dimensions={0}, use_global_device_ids=true | all-gather | bytes 589824 | tf_op jit(solution)/shard_map/all_gather | solution.py:76
  92.6 33.4 %all_gather.38 = bf16[1024,256]{1,0:T(8,128)(2,1)} all-gather(bf16[128,256]{1,0:T(8,128)(2,1)S(1)} %get-tuple-element.29), channel_id=1, replica_groups=mesh['seq'=8,'feat'=4] {'seq'}, dimensions={0}, use_global_device_ids=true | all-gather | bytes 589824 | tf_op jit(solution)/shard_map/all_gather | solution.py:75
  136.5 34.7 %reduce-scatter.5.cloned.1.call-done = f32[32,5120]{1,0:T(8,128)} async-done(((f32[128,5120]{1,0:T(8,128)}), f32[32,5120]{1,0:T(8,128)}) %reduce-scatter.5.cloned.1.call-update) | async-done | bytes 655376 | tf_op jit(solution)/shard_map/reduce_scatter | solution.py:98
  174.9 18.0 %all-gather.7.cloned.1.call-done = bf16[128,5120]{1,0:T(8,128)(2,1)} async-done(((bf16[32,5120]{1,0:T(8,128)(2,1)}), bf16[128,5120]{1,0:T(8,128)(2,1)}) %all-gather.7.cloned.1.call-update) | async-done | bytes 1310736 | tf_op jit(solution)/shard_map/all_gather | solution.py:66
  192.9 9.2 %convolution_convert_fusion.2 = bf16[128,1792]{1,0:T(8,128)(2,1)S(1)} fusion(bf16[128,5120]{1,0:T(8,128)(2,1)} %all-gather.7.cloned.1.call-done, bf16[5120,1792]{1,0:T(8,128)(2,1)} %constant_dynamic-update-slice_fusion), kind=kOutput, calls=%fused_computation.35 | convolution fusion | flops 2349039616 | bytes 20119552 | tf_op jit(solution)/shard_map/dot_general | solution.py:65
  202.8 31.4 %all_gather.40 = bf16[1024,256]{1,0:T(8,128)(2,1)S(1)} all-gather(bf16[128,256]{1,0:T(8,128)(2,1)S(1)} %get-tuple-element.28), channel_id=1, replica_groups=mesh['seq'=8,'feat'=4] {'seq'}, dimensions={0}, use_global_device_ids=true | all-gather | bytes 589824 | tf_op jit(solution)/shard_map/all_gather | solution.py:76
  237.2 33.4 %all_gather.41 = bf16[1024,256]{1,0:T(8,128)(2,1)} all-gather(bf16[128,256]{1,0:T(8,128)(2,1)S(1)} %get-tuple-element.27), channel_id=1, replica_groups=mesh['seq'=8,'feat'=4] {'seq'}, dimensions={0}, use_global_device_ids=true | all-gather | bytes 589824 | tf_op jit(solution)/shard_map/all_gather | solution.py:75
  281.5 34.2 %reduce-scatter.7.cloned.1.call-done = f32[32,5120]{1,0:T(8,128)} async-done(((f32[128,5120]{1,0:T(8,128)}), f32[32,5120]{1,0:T(8,128)}) %reduce-scatter.7.cloned.1.call-update) | async-done | bytes 655376 | tf_op jit(solution)/shard_map/reduce_scatter | solution.py:98
  319.5 12.0 %fusion.48 = f32[2,2]{1,0:T(2,128)S(1)} fusion(f32[2,32,5120]{2,1,0:T(8,128)S(1)} %pad_maximum_fusion.2), kind=kOutput, calls=%fused_computation.47 | convolution fusion | flops 7864320 | bytes 1310736 | tf_op jit(solution)/shard_map/dot_general | solution.py:115
  331.5 39.2 %psum.21 = f32[2,2]{1,0:T(2,128)S(1)} all-reduce(f32[2,2]{1,0:T(2,128)S(1)} %fusion.48), channel_id=1, replica_groups=mesh['seq'=8,'feat'=4] {'seq','feat'}, use_global_device_ids=true, to_apply=%region_10.11 | all-reduce | flops 4 | bytes 32 | tf_op jit(solution)/shard_map/psum | solution.py:116
  379.4 18.8 %all-gather.9.cloned.1.call-done = bf16[128,5120]{1,0:T(8,128)(2,1)} async-done(((bf16[32,5120]{1,0:T(8,128)(2,1)}), bf16[128,5120]{1,0:T(8,128)(2,1)}) %all-gather.9.cloned.1.call-update) | async-done | bytes 1310736 | tf_op jit(solution)/shard_map/all_gather | solution.py:66
  398.2 9.2 %convolution_convert_fusion.1 = bf16[128,1792]{1,0:T(8,128)(2,1)S(1)} fusion(bf16[128,5120]{1,0:T(8,128)(2,1)} %all-gather.9.cloned.1.call-done, bf16[5120,1792]{1,0:T(8,128)(2,1)} %constant_dynamic-update-slice_fusion), kind=kOutput, calls=%fused_computation.34 | convolution fusion | flops 2349039616 | bytes 20119552 | tf_op jit(solution)/shard_map/dot_general | solution.py:65
  408.8 31.5 %all_gather.43 = bf16[1024,256]{1,0:T(8,128)(2,1)S(1)} all-gather(bf16[128,256]{1,0:T(8,128)(2,1)S(1)} %get-tuple-element.26), channel_id=1, replica_groups=mesh['seq'=8,'feat'=4] {'seq'}, dimensions={0}, use_global_device_ids=true | all-gather | bytes 589824 | tf_op jit(solution)/shard_map/all_gather | solution.py:76
  442.4 33.7 %all_gather.44 = bf16[1024,256]{1,0:T(8,128)(2,1)} all-gather(bf16[128,256]{1,0:T(8,128)(2,1)} %get-tuple-element.25), channel_id=1, replica_groups=mesh['seq'=8,'feat'=4] {'seq'}, dimensions={0}, use_global_device_ids=true | all-gather | bytes 589824 | tf_op jit(solution)/shard_map/all_gather | solution.py:75
  485.9 34.5 %reduce-scatter.9.cloned.1.call-done = f32[32,5120]{1,0:T(8,128)} async-done(((f32[128,5120]{1,0:T(8,128)}), f32[32,5120]{1,0:T(8,128)}) %reduce-scatter.9.cloned.1.call-update) | async-done | bytes 655376 | tf_op jit(solution)/shard_map/reduce_scatter | solution.py:98
  525.7 13.0 %fusion.42 = f32[3,3]{1,0:T(4,128)S(1)} fusion(f32[3,32,5120]{2,1,0:T(8,128)S(1)} %pad_maximum_fusion.1), kind=kOutput, calls=%fused_computation.45 | convolution fusion | flops 17694720 | bytes 1966116 | tf_op jit(solution)/shard_map/dot_general | solution.py:115
  538.7 39.2 %psum.22 = f32[3,3]{1,0:T(4,128)S(1)} all-reduce(f32[3,3]{1,0:T(4,128)S(1)} %fusion.42), channel_id=1, replica_groups=mesh['seq'=8,'feat'=4] {'seq','feat'}, use_global_device_ids=true, to_apply=%region_16.17 | all-reduce | flops 9 | bytes 72 | tf_op jit(solution)/shard_map/psum | solution.py:116
  593.7 19.0 %all-gather.11.cloned.1.call-done = bf16[128,5120]{1,0:T(8,128)(2,1)} async-done(((bf16[32,5120]{1,0:T(8,128)(2,1)}), bf16[128,5120]{1,0:T(8,128)(2,1)}) %all-gather.11.cloned.1.call-update) | async-done | bytes 1310736 | tf_op jit(solution)/shard_map/all_gather | solution.py:66
  612.7 9.2 %convolution_convert_fusion = bf16[128,1792]{1,0:T(8,128)(2,1)S(1)} fusion(bf16[128,5120]{1,0:T(8,128)(2,1)} %all-gather.11.cloned.1.call-done, bf16[5120,1792]{1,0:T(8,128)(2,1)} %constant_dynamic-update-slice_fusion), kind=kOutput, calls=%fused_computation.33 | convolution fusion | flops 2349039616 | bytes 20119552 | tf_op jit(solution)/shard_map/dot_general | solution.py:65
  622.7 31.6 %all_gather.46 = bf16[1024,256]{1,0:T(8,128)(2,1)S(1)} all-gather(bf16[128,256]{1,0:T(8,128)(2,1)S(1)} %get-tuple-element.24), channel_id=1, replica_groups=mesh['seq'=8,'feat'=4] {'seq'}, dimensions={0}, use_global_device_ids=true | all-gather | bytes 589824 | tf_op jit(solution)/shard_map/all_gather | solution.py:76
  657.2 33.8 %all_gather.47 = bf16[1024,256]{1,0:T(8,128)(2,1)} all-gather(bf16[128,256]{1,0:T(8,128)(2,1)S(1)} %get-tuple-element.23), channel_id=1, replica_groups=mesh['seq'=8,'feat'=4] {'seq'}, dimensions={0}, use_global_device_ids=true | all-gather | bytes 589824 | tf_op jit(solution)/shard_map/all_gather | solution.py:75
  701.4 34.8 %reduce-scatter.11.cloned.1.call-done = f32[32,5120]{1,0:T(8,128)} async-done(((f32[128,5120]{1,0:T(8,128)}), f32[32,5120]{1,0:T(8,128)}) %reduce-scatter.11.cloned.1.call-update) | async-done | bytes 655376 | tf_op jit(solution)/shard_map/reduce_scatter | solution.py:98
  741.2 13.6 %fusion.45 = f32[4,4]{1,0:T(4,128)S(1)} fusion(f32[4,32,5120]{2,1,0:T(8,128)S(1)} %pad_maximum_fusion), kind=kOutput, calls=%fused_computation.46 | convolution fusion | flops 31457280 | bytes 2621504 | tf_op jit(solution)/shard_map/dot_general | solution.py:115
  754.9 39.2 %psum.23 = f32[4,4]{1,0:T(4,128)S(1)} all-reduce(f32[4,4]{1,0:T(4,128)S(1)} %fusion.45), channel_id=1, replica_groups=mesh['seq'=8,'feat'=4] {'seq','feat'}, use_global_device_ids=true, to_apply=%region_22.23 | all-reduce | flops 16 | bytes 128 | tf_op jit(solution)/shard_map/psum | solution.py:116
  813.3 4.0 multiply_add_fusion
  817.3 13.6 %all_to_all.46 = f32[32,4,1280]{2,0,1:T(8,128)S(1)} all-to-all(f32[32,4,1280]{2,0,1:T(8,128)S(1)} %bitcast.240), channel_id=1, replica_groups=mesh['seq'=8,'feat'=4] {'feat'}, dimensions={1} | all-to-all | bytes 1310720 | tf_op jit(solution)/shard_map/all_to_all | solution.py:121
  (184 shorter events, 99.2 us)
Async XLA Ops:
  6.5 21.6 %copy-start.13 = (f32[5120]{0:T(1024)S(1)}, f32[5120]{0:T(1024)}, u32[]{:S(2)}) copy-start(f32[5120]{0:T(1024)} %param.10) | copy-start | bytes 61444
  17.6 10.1 %all-to-all-start = ((bf16[4,32,1280]{2,1,0:T(8,128)(2,1)}), bf16[4,32,1280]{2,1,0:T(8,128)(2,1)S(1)}, u32[]{:S(2)}, u32[]{:S(2)}) async-start(bf16[4,32,1280]{2,1,0:T(8,128)(2,1)} %bitcast.260), calls=%async_computation | async-start | bytes 655360 | tf_op jit(solution)/shard_map/all_to_all | solution.py:54
  21.1 27.2 %all-gather.5.cloned.1.call-start = ((), (), s32[]{:S(2)}) async-start(), calls=%async_computation.7 | async-start | bytes 1638400 | tf_op jit(solution)/shard_map/all_gather | solution.py:66
  29.0 142.2 %reduce-scatter.5.cloned.1.call-start = ((), (), s32[]{:S(2)}) async-start(), calls=%async_computation.8 | async-start | bytes 3276800 | tf_op jit(solution)/shard_map/reduce_scatter | solution.py:98
  39.9 3.7 copy-start.7
  90.7 41.4 %slice-start = ((s8[13107200]{0:T(1024)(128)(4,1)}), s8[524288]{0:T(1024)(128)(4,1)S(1)}, s32[]{:S(2)}) async-start(s8[13107200]{0:T(1024)(128)(4,1)} %bitcast.226), calls=%async_computation.15 | async-start | bytes 1048576
  127.2 3.4 copy-start.10
  127.2 4.8 slice-start.1
  129.3 2.8 slice-start.2
  130.6 2.4 slice-start.3
  133.0 39.5 %copy-start.8 = (f32[5120]{0:T(1024)S(1)}, f32[5120]{0:T(1024)}, u32[]{:S(2)}) copy-start(f32[5120]{0:T(1024)} %param.11) | copy-start | bytes 61444
  136.4 56.4 %all-gather.7.cloned.1.call-start = ((), (), s32[]{:S(2)}) async-start(), calls=%async_computation.9 | async-start | bytes 1638400 | tf_op jit(solution)/shard_map/all_gather | solution.py:66
  172.8 145.5 %copy-start = (f32[1,32,5120]{2,1,0:T(8,128)}, f32[1,32,5120]{2,1,0:T(8,128)S(1)}, u32[]{:S(2)}) copy-start(f32[1,32,5120]{2,1,0:T(8,128)S(1)} %get-tuple-element.22) | copy-start | bytes 1966084
  174.5 141.2 %reduce-scatter.7.cloned.1.call-start = ((), (), s32[]{:S(2)}) async-start(), calls=%async_computation.10 | async-start | bytes 3276800 | tf_op jit(solution)/shard_map/reduce_scatter | solution.py:98
  235.2 41.4 %slice-start.4 = ((s8[13107200]{0:T(1024)(128)(4,1)}), s8[524288]{0:T(1024)(128)(4,1)S(1)}, s32[]{:S(2)}) async-start(s8[13107200]{0:T(1024)(128)(4,1)} %bitcast.228), calls=%async_computation.19 | async-start | bytes 1048576
  271.8 3.4 copy-start.11
  271.8 4.8 slice-start.5
  273.9 2.8 slice-start.6
  275.1 2.4 slice-start.7
  281.0 117.3 %all-gather.9.cloned.1.call-start = ((), (), s32[]{:S(2)}) async-start(), calls=%async_computation.11 | async-start | bytes 1638400 | tf_op jit(solution)/shard_map/all_gather | solution.py:66
  379.2 141.3 %reduce-scatter.9.cloned.1.call-start = ((), (), s32[]{:S(2)}) async-start(), calls=%async_computation.12 | async-start | bytes 3276800 | tf_op jit(solution)/shard_map/reduce_scatter | solution.py:98
  440.2 40.7 %slice-start.8 = ((s8[13107200]{0:T(1024)(128)(4,1)}), s8[524288]{0:T(1024)(128)(4,1)S(1)}, s32[]{:S(2)}) async-start(s8[13107200]{0:T(1024)(128)(4,1)} %bitcast.230), calls=%async_computation.23 | async-start | bytes 1048576
  477.3 3.7 slice-start.9
  478.2 2.9 slice-start.10
  479.5 2.7 slice-start.11
  485.6 127.1 %all-gather.11.cloned.1.call-start = ((), (), s32[]{:S(2)}) async-start(), calls=%async_computation.13 | async-start | bytes 1638400 | tf_op jit(solution)/shard_map/all_gather | solution.py:66
  593.7 142.5 %reduce-scatter.11.cloned.1.call-start = ((), (), s32[]{:S(2)}) async-start(), calls=%async_computation.14 | async-start | bytes 3276800 | tf_op jit(solution)/shard_map/reduce_scatter | solution.py:98
  622.7 74.3 %slice-start.12 = ((s8[13107200]{0:T(1024)(128)(4,1)}), s8[524288]{0:T(1024)(128)(4,1)S(1)}, s32[]{:S(2)}) async-start(s8[13107200]{0:T(1024)(128)(4,1)} %bitcast.232), calls=%async_computation.27 | async-start | bytes 1048576
  692.1 3.4 copy-start.9
  692.1 4.8 slice-start.13
  694.2 2.8 slice-start.14
  701.4 38.4 %copy-start.1 = (f32[1,32,5120]{2,1,0:T(8,128)S(1)}, f32[1,32,5120]{2,1,0:T(8,128)}, u32[]{:S(2)}) copy-start(f32[1,32,5120]{2,1,0:T(8,128)} %copy-done) | copy-start | bytes 1966084
  (7 other events, 8.9 us)
Sparse Core Ops, SparseCore 0:
  29.1 19.0 all-gather.4
  136.5 34.6 reduce-scatter.4
  174.7 18.1 all-gather.6
  281.1 34.6 reduce-scatter.6
  379.3 18.8 all-gather.8
  485.8 34.6 reduce-scatter.8
  593.8 18.8 all-gather.10
  701.5 34.6 reduce-scatter.10
where the time goes:
time: 848 us; the launch traced here: 839 us
  blocking collectives  403 us (48%)
  waiting for transfers between devices  204 us (24%)
  matrix products  102 us (12%)
  local copies, waits for them, and re-layouts  54.8 us (6%)
  between operations  39 us (5%)
  other arithmetic  31.9 us (4%)
    reduce_scatter x4, waiting for transfers between devices, on_device(): lax.psum_scatter(jnp.dot(attended, w_out, preferred_element_type=jnp.floa...  138 us
    all_gather x4, blocking collectives, on_device(): key_piece = lax.all_gather(key_rows, 'seq', axis=0, tiled=True)  134 us
    all_gather x4, blocking collectives, on_device(): value_piece = lax.all_gather(value_rows, 'seq', axis=0, tiled=True)  126 us
    psum x3, blocking collectives, on_device(): gram_matrix = lax.psum(local_gram, ('seq', 'feat'))  118 us
    all_gather x4, waiting for transfers between devices, on_device(): lax.all_gather(normed, 'feat', axis=0, tiled=True)  58.7 us
    dot_general x3, matrix products, on_device(): local_gram = jnp.dot(stacked, stacked.T, precision=lax.Precision.HIGHEST)  38.6 us
    dot_general x4, matrix products, on_device(): jnp.dot(lax.all_gather(normed, 'feat', axis=0, tiled=True), w_joined, pre...  36.7 us
    unnamed x63, local copies, waits for them, and re-layouts  23.7 us
  transfers between devices with their start and end apart: 9, of which 9 were waited for; matrix products, arithmetic and copies ran while one was open for 2% of the time, Pallas kernels for 0%

commit v1 on v0

--- a/solution.py
+++ b/solution.py
@@ -72,8 +72,13 @@
         value_rows = layer_joined[:, head_cols + kv_cols :]
         start_max = jnp.full((tok_dev, kv_local, group), -1e30, jnp.float32)
         run_max = start_max
-        key_piece = lax.all_gather(key_rows, "seq", axis=0, tiled=True)
-        value_piece = lax.all_gather(value_rows, "seq", axis=0, tiled=True)
+        key_piece, value_piece = jnp.split(
+            lax.all_gather(
+                jnp.concatenate([key_rows, value_rows], axis=1), axis=0, axis_name="seq", tiled=True
+            ),
+            [key_rows.shape[1]],
+            axis=1,
+        )
         length = key_piece.shape[0]
         key_heads = key_piece.reshape(length, kv_local, HEAD_DIM)
         value_heads = value_piece.reshape(length, kv_local, HEAD_DIM)

time: 848 us -> 745 us (0.88)
  blocking collectives: 403 us -> 142 us
  waiting for transfers between devices: 204 us -> 357 us
    all_gather x8 -> x0, blocking collectives: 260 us -> none  [the longest x4 134 us: on_device(): key_piece = lax.all_gather(key_rows, 'seq', axis=0, tiled=True)]
    all_gather x0 -> x4, waiting for transfers between devices: none -> 158 us  [on_device(): lax.all_gather(jnp.concatenate([key_rows, value_rows], axis=1), axis=0, a...]
  transfers between devices with their start and end apart: 9 -> 13, of which waited for: 9 -> 13; matrix products, arithmetic and copies ran while one was open for 2% -> 2% of each run, Pallas kernels for 0% -> 0%
where the time goes in v1:
time: 745 us; the launch traced here: 736 us
  waiting for transfers between devices  357 us (48%)
  blocking collectives  142 us (19%)
  matrix products  102 us (14%)
  local copies, waits for them, and re-layouts  56.8 us (8%)
  between operations  39.3 us (5%)
  other arithmetic  33 us (4%)
    all_gather x4, waiting for transfers between devices, on_device(): lax.all_gather(jnp.concatenate([key_rows, value_rows], axis=1), axis=0, a...  158 us
    reduce_scatter x4, waiting for transfers between devices, on_device(): lax.psum_scatter(jnp.dot(attended, w_out, preferred_element_type=jnp.floa...  133 us
    psum x3, blocking collectives, on_device(): gram_matrix = lax.psum(local_gram, ('seq', 'feat'))  118 us
    all_gather x4, waiting for transfers between devices, on_device(): lax.all_gather(normed, 'feat', axis=0, tiled=True)  59.6 us
    dot_general x3, matrix products, on_device(): local_gram = jnp.dot(stacked, stacked.T, precision=lax.Precision.HIGHEST)  38.6 us
    dot_general x4, matrix products, on_device(): jnp.dot(lax.all_gather(normed, 'feat', axis=0, tiled=True), w_joined, pre...  36.7 us
    unnamed x63, local copies, waits for them, and re-layouts  22.1 us
  transfers between devices with their start and end apart: 13, of which 13 were waited for; matrix products, arithmetic and copies ran while one was open for 2% of the time, Pallas kernels for 0%

profile of v1, /device:TPU:0, one launch (start us, length us, event | category | flops | bytes accessed | tf_op | source)
XLA Modules:
  0.0 735.7 jit_solution(2707644298306511193)
XLA Ops:
  6.5 11.1 %all_to_all.45 = bf16[4,32,1280]{2,1,0:T(8,128)(2,1)S(1)} all-to-all(bf16[4,32,1280]{2,1,0:T(8,128)(2,1)} %bitcast.259), channel_id=1, replica_groups=mesh['seq'=8,'feat'=4] {'feat'}, dimensions={0} | all-to-all | bytes 655360 | tf_op jit(solution)/shard_map/all_to_all | solution.py:53
  17.6 3.5 all-to-all-start
  21.3 6.5 all-to-all-done
  29.1 11.1 %constant_dynamic-update-slice_fusion.2 = bf16[5120,1792]{1,0:T(8,128)(2,1)} fusion(bf16[5120,1280]{1,0:T(8,128)(2,1)} %param.12), kind=kLoop, calls=%fused_computation.95 | loop fusion | bytes 26214400
  44.6 3.7 all-gather.9.cloned.1.call-done
  48.3 9.2 %convolution_convert_fusion.3 = bf16[128,1792]{1,0:T(8,128)(2,1)S(1)} fusion(bf16[128,5120]{1,0:T(8,128)(2,1)} %all-gather.9.cloned.1.call-done, bf16[5120,1792]{1,0:T(8,128)(2,1)} %constant_dynamic-update-slice_fusion), kind=kOutput, calls=%fused_computation.36 | convolution fusion | flops 2349039616 | bytes 20119552 | tf_op jit(solution)/shard_map/dot_general | solution.py:65
  59.2 39.3 %all-gather.11.cloned.1.call-done = bf16[1024,512]{1,0:T(8,128)(2,1)} async-done(((bf16[128,512]{1,0:T(8,128)(2,1)}), bf16[1024,512]{1,0:T(8,128)(2,1)}) %all-gather.11.cloned.1.call-update) | async-done | bytes 1048592 | tf_op jit(solution)/shard_map/all_gather | solution.py:76
  108.6 3.4 fusion.115
  112.1 33.3 %reduce-scatter.5.cloned.1.call-done = f32[32,5120]{1,0:T(8,128)} async-done(((f32[128,5120]{1,0:T(8,128)}), f32[32,5120]{1,0:T(8,128)}) %reduce-scatter.5.cloned.1.call-update) | async-done | bytes 655376 | tf_op jit(solution)/shard_map/reduce_scatter | solution.py:103
  149.1 18.0 %all-gather.13.cloned.1.call-done = bf16[128,5120]{1,0:T(8,128)(2,1)} async-done(((bf16[32,5120]{1,0:T(8,128)(2,1)}), bf16[128,5120]{1,0:T(8,128)(2,1)}) %all-gather.13.cloned.1.call-update) | async-done | bytes 1310736 | tf_op jit(solution)/shard_map/all_gather | solution.py:66
  167.0 9.2 %convolution_convert_fusion.2 = bf16[128,1792]{1,0:T(8,128)(2,1)S(1)} fusion(bf16[128,5120]{1,0:T(8,128)(2,1)} %all-gather.13.cloned.1.call-done, bf16[5120,1792]{1,0:T(8,128)(2,1)} %constant_dynamic-update-slice_fusion), kind=kOutput, calls=%fused_computation.35 | convolution fusion | flops 2349039616 | bytes 20119552 | tf_op jit(solution)/shard_map/dot_general | solution.py:65
  177.9 39.4 %all-gather.15.cloned.1.call-done = bf16[1024,512]{1,0:T(8,128)(2,1)} async-done(((bf16[128,512]{1,0:T(8,128)(2,1)}), bf16[1024,512]{1,0:T(8,128)(2,1)}) %all-gather.15.cloned.1.call-update) | async-done | bytes 1048592 | tf_op jit(solution)/shard_map/all_gather | solution.py:76
  227.4 3.4 fusion.116
  231.4 32.8 %reduce-scatter.7.cloned.1.call-done = f32[32,5120]{1,0:T(8,128)} async-done(((f32[128,5120]{1,0:T(8,128)}), f32[32,5120]{1,0:T(8,128)}) %reduce-scatter.7.cloned.1.call-update) | async-done | bytes 655376 | tf_op jit(solution)/shard_map/reduce_scatter | solution.py:103
  267.9 12.0 %fusion.48 = f32[2,2]{1,0:T(2,128)S(1)} fusion(f32[2,32,5120]{2,1,0:T(8,128)S(1)} %pad_maximum_fusion.2), kind=kOutput, calls=%fused_computation.47 | convolution fusion | flops 7864320 | bytes 1310736 | tf_op jit(solution)/shard_map/dot_general | solution.py:120
  279.9 39.2 %psum.21 = f32[2,2]{1,0:T(2,128)S(1)} all-reduce(f32[2,2]{1,0:T(2,128)S(1)} %fusion.48), channel_id=1, replica_groups=mesh['seq'=8,'feat'=4] {'seq','feat'}, use_global_device_ids=true, to_apply=%region_10.11 | all-reduce | flops 4 | bytes 32 | tf_op jit(solution)/shard_map/psum | solution.py:121
  327.7 18.9 %all-gather.17.cloned.1.call-done = bf16[128,5120]{1,0:T(8,128)(2,1)} async-done(((bf16[32,5120]{1,0:T(8,128)(2,1)}), bf16[128,5120]{1,0:T(8,128)(2,1)}) %all-gather.17.cloned.1.call-update) | async-done | bytes 1310736 | tf_op jit(solution)/shard_map/all_gather | solution.py:66
  346.6 9.2 %convolution_convert_fusion.1 = bf16[128,1792]{1,0:T(8,128)(2,1)S(1)} fusion(bf16[128,5120]{1,0:T(8,128)(2,1)} %all-gather.17.cloned.1.call-done, bf16[5120,1792]{1,0:T(8,128)(2,1)} %constant_dynamic-update-slice_fusion), kind=kOutput, calls=%fused_computation.34 | convolution fusion | flops 2349039616 | bytes 20119552 | tf_op jit(solution)/shard_map/dot_general | solution.py:65
  356.8 40.1 %all-gather.19.cloned.1.call-done = bf16[1024,512]{1,0:T(8,128)(2,1)} async-done(((bf16[128,512]{1,0:T(8,128)(2,1)}), bf16[1024,512]{1,0:T(8,128)(2,1)}) %all-gather.19.cloned.1.call-update) | async-done | bytes 1048592 | tf_op jit(solution)/shard_map/all_gather | solution.py:76
  406.2 3.4 fusion.117
  409.9 33.1 %reduce-scatter.9.cloned.1.call-done = f32[32,5120]{1,0:T(8,128)} async-done(((f32[128,5120]{1,0:T(8,128)}), f32[32,5120]{1,0:T(8,128)}) %reduce-scatter.9.cloned.1.call-update) | async-done | bytes 655376 | tf_op jit(solution)/shard_map/reduce_scatter | solution.py:103
  448.2 13.0 %fusion.42 = f32[3,3]{1,0:T(4,128)S(1)} fusion(f32[3,32,5120]{2,1,0:T(8,128)S(1)} %pad_maximum_fusion.1), kind=kOutput, calls=%fused_computation.45 | convolution fusion | flops 17694720 | bytes 1966116 | tf_op jit(solution)/shard_map/dot_general | solution.py:120
  461.2 39.3 %psum.22 = f32[3,3]{1,0:T(4,128)S(1)} all-reduce(f32[3,3]{1,0:T(4,128)S(1)} %fusion.42), channel_id=1, replica_groups=mesh['seq'=8,'feat'=4] {'seq','feat'}, use_global_device_ids=true, to_apply=%region_16.17 | all-reduce | flops 9 | bytes 72 | tf_op jit(solution)/shard_map/psum | solution.py:121
  517.0 19.0 %all-gather.21.cloned.1.call-done = bf16[128,5120]{1,0:T(8,128)(2,1)} async-done(((bf16[32,5120]{1,0:T(8,128)(2,1)}), bf16[128,5120]{1,0:T(8,128)(2,1)}) %all-gather.21.cloned.1.call-update) | async-done | bytes 1310736 | tf_op jit(solution)/shard_map/all_gather | solution.py:66
  536.1 9.2 %convolution_convert_fusion = bf16[128,1792]{1,0:T(8,128)(2,1)S(1)} fusion(bf16[128,5120]{1,0:T(8,128)(2,1)} %all-gather.21.cloned.1.call-done, bf16[5120,1792]{1,0:T(8,128)(2,1)} %constant_dynamic-update-slice_fusion), kind=kOutput, calls=%fused_computation.33 | convolution fusion | flops 2349039616 | bytes 20119552 | tf_op jit(solution)/shard_map/dot_general | solution.py:65
  547.3 39.0 %all-gather.23.cloned.1.call-done = bf16[1024,512]{1,0:T(8,128)(2,1)} async-done(((bf16[128,512]{1,0:T(8,128)(2,1)}), bf16[1024,512]{1,0:T(8,128)(2,1)}) %all-gather.23.cloned.1.call-update) | async-done | bytes 1048592 | tf_op jit(solution)/shard_map/all_gather | solution.py:76
  596.4 3.4 fusion.118
  599.8 33.4 %reduce-scatter.11.cloned.1.call-done = f32[32,5120]{1,0:T(8,128)} async-done(((f32[128,5120]{1,0:T(8,128)}), f32[32,5120]{1,0:T(8,128)}) %reduce-scatter.11.cloned.1.call-update) | async-done | bytes 655376 | tf_op jit(solution)/shard_map/reduce_scatter | solution.py:103
  638.3 13.6 %fusion.45 = f32[4,4]{1,0:T(4,128)S(1)} fusion(f32[4,32,5120]{2,1,0:T(8,128)S(1)} %pad_maximum_fusion), kind=kOutput, calls=%fused_computation.46 | convolution fusion | flops 31457280 | bytes 2621504 | tf_op jit(solution)/shard_map/dot_general | solution.py:120
  651.9 39.2 %psum.23 = f32[4,4]{1,0:T(4,128)S(1)} all-reduce(f32[4,4]{1,0:T(4,128)S(1)} %fusion.45), channel_id=1, replica_groups=mesh['seq'=8,'feat'=4] {'seq','feat'}, use_global_device_ids=true, to_apply=%region_22.23 | all-reduce | flops 16 | bytes 128 | tf_op jit(solution)/shard_map/psum | solution.py:121
  710.1 4.0 multiply_add_fusion
  714.2 13.6 %all_to_all.46 = f32[32,4,1280]{2,0,1:T(8,128)S(1)} all-to-all(f32[32,4,1280]{2,0,1:T(8,128)S(1)} %bitcast.240), channel_id=1, replica_groups=mesh['seq'=8,'feat'=4] {'feat'}, dimensions={1} | all-to-all | bytes 1310720 | tf_op jit(solution)/shard_map/all_to_all | solution.py:126
  (192 shorter events, 89.8 us)
Async XLA Ops:
  6.5 21.6 %copy-start.13 = (f32[5120]{0:T(1024)S(1)}, f32[5120]{0:T(1024)}, u32[]{:S(2)}) copy-start(f32[5120]{0:T(1024)} %param.10) | copy-start | bytes 61444
  17.6 10.1 %all-to-all-start = ((bf16[4,32,1280]{2,1,0:T(8,128)(2,1)}), bf16[4,32,1280]{2,1,0:T(8,128)(2,1)S(1)}, u32[]{:S(2)}, u32[]{:S(2)}) async-start(bf16[4,32,1280]{2,1,0:T(8,128)(2,1)} %bitcast.260), calls=%async_computation | async-start | bytes 655360 | tf_op jit(solution)/shard_map/all_to_all | solution.py:54
  21.1 27.2 %all-gather.9.cloned.1.call-start = ((), (), s32[]{:S(2)}) async-start(), calls=%async_computation.7 | async-start | bytes 1638400 | tf_op jit(solution)/shard_map/all_gather | solution.py:66
  29.0 69.5 %all-gather.11.cloned.1.call-start = ((), (), s32[]{:S(2)}) async-start(), calls=%async_computation.8 | async-start | bytes 1179648 | tf_op jit(solution)/shard_map/all_gather | solution.py:76
  29.1 11.1 %copy-start.6 = (bf16[5120,256]{1,0:T(8,128)(2,1)S(1)}, bf16[5120,256]{1,0:T(8,128)(2,1)}, u32[]{:S(2)}) copy-start(bf16[5120,256]{1,0:T(8,128)(2,1)} %param.13) | copy-start | bytes 7864324
  58.1 87.3 %reduce-scatter.5.cloned.1.call-start = ((), (), s32[]{:S(2)}) async-start(), calls=%async_computation.9 | async-start | bytes 3276800 | tf_op jit(solution)/shard_map/reduce_scatter | solution.py:103
  100.6 7.0 slice-start
  102.8 3.4 copy-start.10
  102.8 4.8 slice-start.1
  104.9 2.8 slice-start.2
  108.6 38.1 %copy-start.8 = (f32[5120]{0:T(1024)S(1)}, f32[5120]{0:T(1024)}, u32[]{:S(2)}) copy-start(f32[5120]{0:T(1024)} %param.11) | copy-start | bytes 61444
  112.0 55.0 %all-gather.13.cloned.1.call-start = ((), (), s32[]{:S(2)}) async-start(), calls=%async_computation.10 | async-start | bytes 1638400 | tf_op jit(solution)/shard_map/all_gather | solution.py:66
  147.0 119.7 %copy-start = (f32[1,32,5120]{2,1,0:T(8,128)}, f32[1,32,5120]{2,1,0:T(8,128)S(1)}, u32[]{:S(2)}) copy-start(f32[1,32,5120]{2,1,0:T(8,128)S(1)} %get-tuple-element.30) | copy-start | bytes 1966084
  148.7 68.6 %all-gather.15.cloned.1.call-start = ((), (), s32[]{:S(2)}) async-start(), calls=%async_computation.11 | async-start | bytes 1179648 | tf_op jit(solution)/shard_map/all_gather | solution.py:76
  176.9 87.3 %reduce-scatter.7.cloned.1.call-start = ((), (), s32[]{:S(2)}) async-start(), calls=%async_computation.12 | async-start | bytes 3276800 | tf_op jit(solution)/shard_map/reduce_scatter | solution.py:103
  219.4 7.0 slice-start.4
  221.6 3.4 copy-start.11
  221.6 4.8 slice-start.5
  230.8 115.8 %all-gather.17.cloned.1.call-start = ((), (), s32[]{:S(2)}) async-start(), calls=%async_computation.13 | async-start | bytes 1638400 | tf_op jit(solution)/shard_map/all_gather | solution.py:66
  327.5 69.4 %all-gather.19.cloned.1.call-start = ((), (), s32[]{:S(2)}) async-start(), calls=%async_computation.14 | async-start | bytes 1179648 | tf_op jit(solution)/shard_map/all_gather | solution.py:76
  356.5 86.5 %reduce-scatter.9.cloned.1.call-start = ((), (), s32[]{:S(2)}) async-start(), calls=%async_computation.15 | async-start | bytes 3276800 | tf_op jit(solution)/shard_map/reduce_scatter | solution.py:103
  396.9 8.0 %slice-start.8 = ((s8[13107200]{0:T(1024)(128)(4,1)}), s8[524288]{0:T(1024)(128)(4,1)S(1)}, s32[]{:S(2)}) async-start(s8[13107200]{0:T(1024)(128)(4,1)} %bitcast.230), calls=%async_computation.27 | async-start | bytes 1048576
  401.2 3.7 slice-start.9
  402.2 2.9 slice-start.10
  409.6 126.4 %all-gather.21.cloned.1.call-start = ((), (), s32[]{:S(2)}) async-start(), calls=%async_computation.16 | async-start | bytes 1638400 | tf_op jit(solution)/shard_map/all_gather | solution.py:66
  517.0 69.4 %all-gather.23.cloned.1.call-start = ((), (), s32[]{:S(2)}) async-start(), calls=%async_computation.17 | async-start | bytes 1179648 | tf_op jit(solution)/shard_map/all_gather | solution.py:76
  545.9 87.3 %reduce-scatter.11.cloned.1.call-start = ((), (), s32[]{:S(2)}) async-start(), calls=%async_computation.18 | async-start | bytes 3276800 | tf_op jit(solution)/shard_map/reduce_scatter | solution.py:103
  586.3 9.1 %slice-start.12 = ((s8[13107200]{0:T(1024)(128)(4,1)}), s8[524288]{0:T(1024)(128)(4,1)S(1)}, s32[]{:S(2)}) async-start(s8[13107200]{0:T(1024)(128)(4,1)} %bitcast.232), calls=%async_computation.31 | async-start | bytes 1048576
  590.6 3.4 copy-start.9
  590.6 4.8 slice-start.13
  592.7 2.8 slice-start.14
  599.8 37.0 %copy-start.1 = (f32[1,32,5120]{2,1,0:T(8,128)S(1)}, f32[1,32,5120]{2,1,0:T(8,128)}, u32[]{:S(2)}) copy-start(f32[1,32,5120]{2,1,0:T(8,128)} %copy-done) | copy-start | bytes 1966084
  (11 other events, 21.2 us)
Sparse Core Ops, SparseCore 0:
  29.1 19.0 all-gather.8
  58.3 40.2 all-gather.10
  112.1 33.2 reduce-scatter.4
  148.9 18.1 all-gather.12
  177.0 40.2 all-gather.14
  230.9 33.2 reduce-scatter.6
  327.6 18.9 all-gather.16
  356.6 40.2 all-gather.18
  409.7 33.2 reduce-scatter.8
  517.1 18.9 all-gather.20
  546.0 40.2 all-gather.22
  600.0 33.2 reduce-scatter.10
